TPU v7x, 32 devices: a whole 2x2x4 slice. The times are simulated.
32 devices in a mesh: chan: 4 (over y, x), slab: 8 (over z, core).
Axes of the slice: x: 2, y: 2, z: 4, core: 2. Of those that a mesh axis runs over, the one named last changes fastest.
Arguments:
- taylor_models: float32 [2, 2048, 2048], P(None, 'slab', 'chan'), may hold values from -6 to 6
- gridded_vis: bfloat16 [4, 2, 2048, 2048], P('chan', None, 'slab'), may hold values from -6 to 6
- uv_weight: bfloat16 [4, 2048, 2048], P('chan', 'slab'), may hold values from 0 to 2
- freq_ratio: float32 [4], P('chan'), may hold values from 0.6 to 1.4
- robust_scale: float32 [4], P('chan'), may hold values from 0.25 to 4
Outputs:
- taylor_residual: float32 [2, 2048, 2048], P(None, 'slab', 'chan')
All inputs are finite; a program needn't handle non-finite values.
Results may differ from a plain program's by a relative error of at most 0.0003.
Values sent between devices are 32-bit elements; how exact they have to be, the bound alone decides.
A program may use at most 64 MiB of HBM per device.

v0:
```python
import functools
import math

import jax
import jax.numpy as jnp
import numpy as np
from jax import lax
from jax.experimental import pallas as pl
from jax.experimental.pallas import tpu as pltpu
from jax.sharding import PartitionSpec as P

PIX = 2048
TERMS = 2


HIGHEST = lax.Precision.HIGH


def dft_table(points, direction):
    steps_all = jnp.arange(points, dtype=jnp.int32)
    product = steps_all[:, None] * steps_all[None, :] % points
    angles = product.astype(jnp.float32) * (2.0 * math.pi / points)
    return (jnp.cos(angles), direction * jnp.sin(angles))


def twiddle_table(outer_points, inner_points, direction):
    outer_steps = jnp.arange(outer_points, dtype=jnp.int32)
    inner_steps = jnp.arange(inner_points, dtype=jnp.int32)
    overall = outer_points * inner_points
    product = outer_steps[:, None] * inner_steps[None, :] % overall
    angles = product.astype(jnp.float32) * (2.0 * math.pi / overall)
    return (jnp.cos(angles), direction * jnp.sin(angles))


def complex_product(formula, left_real, left_imag, table_real, table_imag):
    out_real = jnp.einsum(formula, left_real, table_real, precision=HIGHEST) - jnp.einsum(
        formula, left_imag, table_imag, precision=HIGHEST
    )
    out_imag = jnp.einsum(formula, left_real, table_imag, precision=HIGHEST) + jnp.einsum(
        formula, left_imag, table_real, precision=HIGHEST
    )
    return (out_real, out_imag)


def rotate(left_real, left_imag, table_real, table_imag):
    return (
        left_real * table_real - left_imag * table_imag,
        left_real * table_imag + left_imag * table_real,
    )


def local_general(taylor_models, gridded_vis, uv_weight, freq_ratio, robust_scale):
    inner_count = 128
    outer_count = PIX // inner_count
    chans = lax.axis_size("chan")
    slabs = lax.axis_size("slab")
    rows = taylor_models.shape[1]
    cols = taylor_models.shape[2]
    sub = rows // chans
    col_count = PIX // slabs
    outer_cos, outer_sin = dft_table(outer_count, -1.0)
    inner_cos, inner_sin = dft_table(inner_count, -1.0)
    twist_cos, twist_sin = twiddle_table(outer_count, inner_count, -1.0)
    offsets = lax.all_gather(freq_ratio, "chan", axis=0, tiled=True) - 1.0

    pieces = taylor_models.reshape(TERMS, chans, sub, cols).transpose(1, 0, 2, 3)
    pieces = lax.all_to_all(pieces, "chan", split_axis=0, concat_axis=0, tiled=True)
    layered = pieces.transpose(1, 2, 0, 3).reshape(TERMS * sub, outer_count, inner_count)
    part_real = jnp.einsum("yba,jb->yja", layered, outer_cos, precision=HIGHEST)
    part_imag = jnp.einsum("yba,jb->yja", layered, outer_sin, precision=HIGHEST)
    turned_real, turned_imag = rotate(part_real, part_imag, twist_cos, twist_sin)
    spec_real, spec_imag = complex_product(
        "yja,ka->kjy", turned_real, turned_imag, inner_cos, inner_sin
    )
    outgoing = jnp.stack(
        [
            spec_real.reshape(slabs, col_count, TERMS * sub),
            spec_imag.reshape(slabs, col_count, TERMS * sub),
        ],
        axis=1,
    )
    arrived = lax.all_to_all(outgoing, "slab", split_axis=0, concat_axis=0, tiled=True)
    arrived = arrived.reshape(slabs, 2, col_count, TERMS, sub)
    arrived = arrived.transpose(3, 1, 2, 0, 4).reshape(TERMS, 2, col_count, slabs * sub)
    mixed = arrived[0][None] + offsets[:, None, None, None] * arrived[1][None]
    mixed = lax.all_to_all(mixed, "chan", split_axis=0, concat_axis=0, tiled=True)
    columns = mixed.reshape(chans, 2, col_count, slabs, sub).transpose(1, 2, 3, 0, 4)
    layered_cols = columns.reshape(2, col_count, outer_count, inner_count)
    part_real, part_imag = complex_product(
        "uba,jb->uja", layered_cols[0], layered_cols[1], outer_cos, outer_sin
    )
    turned_real, turned_imag = rotate(part_real, part_imag, twist_cos, twist_sin)
    freq_real, freq_imag = complex_product(
        "uja,ka->ujk", turned_real, turned_imag, inner_cos, inner_sin
    )
    freq_real = freq_real / PIX
    freq_imag = freq_imag / PIX
    weight = (
        uv_weight[0]
        .astype(jnp.float32)
        .reshape(col_count, inner_count, outer_count)
        .transpose(0, 2, 1)
    )
    visible = (
        gridded_vis[0]
        .astype(jnp.float32)
        .reshape(2, col_count, inner_count, outer_count)
        .transpose(0, 1, 3, 2)
    )
    delta_real = visible[0] - weight * freq_real
    delta_imag = visible[1] - weight * freq_imag
    robust = 1.0 / (1.0 + robust_scale[0] * (delta_real * delta_real + delta_imag * delta_imag))
    weighted_real = robust * delta_real
    weighted_imag = robust * delta_imag
    back_real, back_imag = complex_product(
        "ujk,ak->uja", weighted_real, weighted_imag, inner_cos, -inner_sin
    )
    back_real, back_imag = rotate(back_real, back_imag, twist_cos, -twist_sin)
    back_real, back_imag = complex_product(
        "uja,bj->uba", back_real, back_imag, outer_cos, -outer_sin
    )
    back = jnp.stack([back_real, back_imag]).reshape(2, col_count, slabs, chans, sub)
    back = back.transpose(3, 0, 1, 2, 4).reshape(chans, 2, col_count, slabs * sub)
    back = lax.all_to_all(back, "chan", split_axis=0, concat_axis=0, tiled=True)
    total = jnp.stack(
        [jnp.sum(back * offsets[:, None, None, None] ** t, axis=0) for t in range(TERMS)]
    )
    total = total.reshape(TERMS, 2, col_count, slabs, sub).transpose(3, 1, 2, 0, 4)
    total = total.reshape(slabs, 2, col_count, TERMS * sub)
    total = lax.all_to_all(total, "slab", split_axis=0, concat_axis=0, tiled=True)
    layered_rows = total.transpose(1, 0, 2, 3).reshape(2, inner_count, outer_count, TERMS * sub)
    last_real, last_imag = complex_product(
        "kjy,ak->ajy", layered_rows[0], layered_rows[1], inner_cos, -inner_sin
    )
    last_real, last_imag = rotate(
        last_real, last_imag, twist_cos.T[:, :, None], -twist_sin.T[:, :, None]
    )
    image_out = jnp.einsum("ajy,bj->yba", last_real, outer_cos, precision=HIGHEST) + jnp.einsum(
        "ajy,bj->yba", last_imag, outer_sin, precision=HIGHEST
    )
    image_out = image_out.reshape(TERMS, sub, chans, cols).transpose(2, 0, 1, 3) / PIX
    tiles = lax.all_to_all(image_out, "chan", split_axis=0, concat_axis=0, tiled=True)
    return tiles.transpose(1, 0, 2, 3).reshape(TERMS, rows, cols)


CHUNKS = 4
GROUP = 8
MESH = pl.DeviceIdType.MESH


def lane_tables(slabs, chans, sub):
    j = np.arange(chans)[:, None, None, None]
    v0 = np.arange(slabs)[None, :, None, None]
    r = np.arange(sub)[None, None, :, None]
    k = np.arange(sub)[None, None, None, :]
    phase = ((chans * r + j) * (v0 + slabs * k)) % PIX
    cos = np.cos(2.0 * np.pi * phase / PIX) / PIX
    sin = -np.sin(2.0 * np.pi * phase / PIX) / PIX
    top = np.concatenate([cos, sin], axis=3)
    low = np.concatenate([-sin, cos], axis=3)
    table = np.concatenate([top, low], axis=2).reshape(chans * slabs, 2 * sub, 2 * sub)
    table = table.astype(np.float32)
    high = table.astype(jnp.bfloat16)
    return high, (table - high.astype(np.float32)).astype(jnp.bfloat16)


def column_tables(slabs, chans, span):
    u1 = np.arange(span).reshape(slabs, CHUNKS, span // (slabs * CHUNKS))
    u1 = u1.transpose(1, 0, 2).reshape(span, 1)
    angle = 2.0 * np.pi * ((u1 * np.arange(span)[None, :]) % span) / span
    table = np.concatenate([np.cos(angle), np.sin(angle)], axis=1).astype(np.float32)
    high = table.astype(jnp.bfloat16)
    low = (table - high.astype(np.float32)).astype(jnp.bfloat16)
    turn = 2.0 * np.pi * np.arange(chans)[:, None] * np.arange(span)[None, :] / PIX
    turn = np.stack([np.cos(turn), np.sin(turn)], axis=1).reshape(2 * chans, span)
    return high, low, turn.astype(np.float32)


def sort_table(slabs, sub):
    span = slabs * sub
    source = jnp.arange(2 * span, dtype=jnp.int32)
    part, v = source // span, source % span
    target = (v % slabs) * (2 * sub) + part * sub + v // slabs
    return (target[:, None] == jnp.arange(2 * span, dtype=jnp.int32)[None, :]).astype(jnp.bfloat16)


def middle_kernel(
    slabs, chans, m_ref, vis_ref, wt_ref, off_ref, rs_ref, high_ref, low_ref, sort_ref,
    xhigh_ref, xlow_ref, turn_ref, out_ref,
    stage, xsend, xrecv, ohigh, olow, acc, rsend, rrecv, g_ref, q_ref, zin, mix, spec, back, landed, qsend, offs, work, vsort, wsort,
    z_send, z_recv, c_send, c_recv, b_send, b_recv, q_send, q_recv, o_send, o_recv,
    x_send, x_recv, r_send, r_recv,
):
    slab = lax.axis_index("slab")
    chan = lax.axis_index("chan")
    unit = g_ref.shape[3]
    lanes = g_ref.shape[4]
    half = lanes // 2
    span = slabs * half

    def slab_peer(d):
        return lax.rem(slab + d, slabs)

    def slab_from(d):
        return lax.rem(slab + slabs - d, slabs)

    def chan_peer(d):
        return lax.rem(chan + d, chans)

    def chan_from(d):
        return lax.rem(chan + chans - d, chans)

    def z_copy(c, d, owner):
        return pltpu.make_async_remote_copy(
            src_ref=g_ref.at[c, slab_peer(d)], dst_ref=zin.at[c, owner],
            send_sem=z_send.at[c, d], recv_sem=z_recv.at[c, d],
            device_id=(chan, slab_peer(d)), device_id_type=MESH)

    def c_copy(c, d, owner):
        return pltpu.make_async_remote_copy(
            src_ref=mix.at[c, d - 1], dst_ref=spec.at[c, owner],
            send_sem=c_send.at[c, d], recv_sem=c_recv.at[c, d],
            device_id=(chan_peer(d), slab), device_id_type=MESH)

    def b_copy(c, d, owner):
        return pltpu.make_async_remote_copy(
            src_ref=back.at[c, d - 1], dst_ref=landed.at[c, owner],
            send_sem=b_send.at[c, d], recv_sem=b_recv.at[c, d],
            device_id=(chan_peer(d), slab), device_id_type=MESH)

    def q_copy(c, d, owner):
        return pltpu.make_async_remote_copy(
            src_ref=qsend.at[c, slab_peer(d)], dst_ref=q_ref.at[c, owner],
            send_sem=q_send.at[c, d], recv_sem=q_recv.at[c, d],
            device_id=(chan, slab_peer(d)), device_id_type=MESH)

    def o_copy(d, owner):
        return pltpu.make_async_remote_copy(
            src_ref=off_ref, dst_ref=offs.at[owner],
            send_sem=o_send.at[d], recv_sem=o_recv.at[d],
            device_id=(chan_peer(d), slab), device_id_type=MESH)

    def x_copy(d, owner):
        return pltpu.make_async_remote_copy(
            src_ref=xsend.at[chan_peer(d)], dst_ref=xrecv.at[owner],
            send_sem=x_send.at[d], recv_sem=x_recv.at[d],
            device_id=(chan_peer(d), slab), device_id_type=MESH)

    def r_copy(d, owner):
        return pltpu.make_async_remote_copy(
            src_ref=rsend.at[chan_peer(d)], dst_ref=rrecv.at[owner],
            send_sem=r_send.at[d], recv_sem=r_recv.at[d],
            device_id=(chan_peer(d), slab), device_id_type=MESH)

    sub = half
    cols = m_ref.shape[2]
    quarter = unit // chans
    for m in range(TERMS):
        for q in range(cols // lanes):
            at = pl.ds(q * lanes, lanes)
            stage[q, m] = m_ref[m, :, at]
            for j in range(chans):
                xsend[j, m, :, at] = stage[q, m, pl.ds(j, sub, stride=chans), :]

    barrier = pltpu.get_barrier_semaphore()
    for d in range(1, slabs):
        pl.semaphore_signal(barrier, inc=1, device_id=(chan, slab_peer(d)), device_id_type=MESH)
    for d in range(1, chans):
        pl.semaphore_signal(barrier, inc=1, device_id=(chan_peer(d), slab), device_id_type=MESH)
    pl.semaphore_wait(barrier, slabs + chans - 2)

    for d in range(1, chans):
        x_copy(d, chan).start()
    for d in range(1, chans):
        o_copy(d, chan).start()

    offs[chan] = off_ref[...]
    xrecv[chan] = xsend[chan]
    acc[...] = jnp.zeros_like(acc)

    @pl.loop(0, CHUNKS)
    def _(c):
        rows = pl.ds(pl.multiple_of(c * unit, unit), unit)
        for jj in range(chans):
            at = pl.ds(jj * span, span)
            pair = jnp.concatenate([vis_ref[0, rows, at], vis_ref[1, rows, at]], axis=1)
            vsort[c, jj] = jnp.dot(pair, sort_ref[...], preferred_element_type=jnp.float32)
            pair = jnp.concatenate([wt_ref[rows, at], wt_ref[rows, at]], axis=1)
            wsort[c, jj] = jnp.dot(pair, sort_ref[...], preferred_element_type=jnp.float32)

    for d in range(1, chans):
        o_copy(d, chan_from(d)).wait_recv()

    for d in range(1, chans):
        x_copy(d, chan_from(d)).wait_recv()

    def halves(x):
        high = x.astype(jnp.bfloat16)
        return high, (x - high.astype(jnp.float32)).astype(jnp.bfloat16)

    for m in range(TERMS):
        @pl.loop(0, sub // 16)
        def _(i):
            start = pl.multiple_of(i * 16, 16)
            x = [xrecv[c, m, pl.ds(start, 16), :] for c in range(chans)]
            s0, s1, t0, t1 = x[0] + x[2], x[0] - x[2], x[1] + x[3], x[1] - x[3]
            for u0 in range(chans):
                cos, sin = turn_ref[2 * u0 : 2 * u0 + 1, :], turn_ref[2 * u0 + 1 : 2 * u0 + 2, :]
                if u0 % 2 == 0:
                    zr = s0 + t0 if u0 == 0 else s0 - t0
                    real, imag = zr * cos, -(zr * sin)
                else:
                    zi = -t1 if u0 == 1 else t1
                    real, imag = s1 * cos + zi * sin, zi * cos - s1 * sin
                one = pl.ds(pl.multiple_of(m * lanes + i * 16, 16), 16)
                two = pl.ds(pl.multiple_of(m * lanes + half + i * 16, 16), 16)
                left, right = pl.ds(0, cols), pl.ds(cols, cols)
                rh, rl = halves(real)
                ih, il = halves(imag)
                for into, re, im in ((ohigh, rh, ih), (olow, rl, il)):
                    into[u0, one, left] = re
                    into[u0, one, right] = im
                    into[u0, two, left] = im
                    into[u0, two, right] = -re

    @pl.loop(0, CHUNKS)
    def _(c):
        at = pl.ds(pl.multiple_of(c * slabs * quarter, slabs * quarter), slabs * quarter)
        th, tl = xhigh_ref[at, :], xlow_ref[at, :]
        dot = functools.partial(
            lax.dot_general, dimension_numbers=(((1,), (1,)), ((), ())),
            preferred_element_type=jnp.float32)
        for u0 in range(chans):
            found = dot(th, ohigh[u0]) + (dot(tl, ohigh[u0]) + dot(th, olow[u0]))
            for s in range(slabs):
                for m in range(TERMS):
                    g_ref[c, s, m, pl.ds(u0, quarter, stride=chans), :] = found[
                        s * quarter : (s + 1) * quarter, m * lanes : (m + 1) * lanes
                    ]
        for d in range(1, slabs):
            z_copy(c, d, slab).start()
        zin[c, slab] = g_ref[c, slab]

    lane = lax.broadcasted_iota(jnp.int32, (GROUP, lanes), 1)
    sign = jnp.where(lane < half, -1.0, 1.0)

    def times_i(x, direction):
        return pltpu.roll(x, half, 1) * (sign * direction)

    def four(x0, x1, x2, x3, direction):
        s0, s1, t0, t1 = x0 + x2, x0 - x2, x1 + x3, times_i(x1 - x3, direction)
        return s0 + t0, s1 + t1, s0 - t0, s1 - t1

    def eight(x, direction):
        root = math.sqrt(0.5)
        even = four(x[0], x[2], x[4], x[6], direction)
        odd = four(x[1], x[3], x[5], x[7], direction)
        odd = (
            odd[0],
            (odd[1] + times_i(odd[1], direction)) * root,
            times_i(odd[2], direction),
            (times_i(odd[3], direction) - odd[3]) * root,
        )
        return [e + o for e, o in zip(even, odd)] + [e - o for e, o in zip(even, odd)]

    def split(x):
        high = x.astype(jnp.bfloat16)
        return high, (x - high.astype(jnp.float32)).astype(jnp.bfloat16)

    def product(x, t, dims):
        high, low = split(x)
        dot = functools.partial(
            lax.dot_general, dimension_numbers=(dims, ((), ())),
            preferred_element_type=jnp.float32)
        wide = dot(high, high_ref[t])
        return wide + (dot(low, high_ref[t]) + dot(high, low_ref[t]))

    def spread(c):
        for d in range(1, slabs):
            z_copy(c, d, slab_from(d)).wait_recv()

        @pl.loop(0, slabs)
        def _(s):
            base, slope = zin[c, s, 0], zin[c, s, 1]
            spec[c, chan, s] = base + offs[chan][0:1, :] * slope
            for d in range(1, chans):
                mix[c, d - 1, s] = base + offs[chan_peer(d)][0:1, :] * slope

        for d in range(1, chans):
            c_copy(c, d, chan).start()

    def weigh(c):
        for d in range(1, chans):
            c_copy(c, d, chan_from(d)).wait_recv()
        damping = rs_ref[0:1, :]

        @pl.loop(0, unit // GROUP)
        def _(i):
            rows = pl.ds(pl.multiple_of(i * GROUP, GROUP), GROUP)
            for j in range(chans):
                out = eight([spec[c, j, s, rows, :] for s in range(slabs)], -1.0)
                for v0 in range(slabs):
                    work[j * slabs + v0, rows, :] = out[v0]

        @pl.loop(0, chans * slabs)
        def _(t):
            work[t] = product(work[t], t, ((1,), (0,)))

        @pl.loop(0, unit // GROUP)
        def _(i):
            rows = pl.ds(pl.multiple_of(i * GROUP, GROUP), GROUP)
            for v0 in range(slabs):
                at = pl.ds(v0 * lanes, lanes)
                found = four(*[work[j * slabs + v0, rows, :] for j in range(chans)], -1.0)
                kept = []
                for jj in range(chans):
                    delta = vsort[c, jj, rows, at] - wsort[c, jj, rows, at] * found[jj]
                    power = delta * delta
                    power = power + pltpu.roll(power, half, 1)
                    kept.append(delta / (1.0 + damping * power))
                out = four(*kept, 1.0)
                for j in range(chans):
                    work[j * slabs + v0, rows, :] = out[j]

        @pl.loop(0, chans * slabs)
        def _(t):
            work[t] = product(work[t], t, ((1,), (1,)))

        @pl.loop(0, unit // GROUP)
        def _(i):
            rows = pl.ds(pl.multiple_of(i * GROUP, GROUP), GROUP)
            for d in range(chans):
                first = chan_peer(d) * slabs
                out = eight([work[first + v0, rows, :] for v0 in range(slabs)], 1.0)
                for s in range(slabs):
                    if d == 0:
                        landed[c, chan, s, rows, :] = out[s]
                    else:
                        back[c, d - 1, s, rows, :] = out[s]

        for d in range(1, chans):
            b_copy(c, d, chan).start()

    def gather(c):
        for d in range(1, chans):
            b_copy(c, d, chan_from(d)).wait_recv()

        @pl.loop(0, slabs)
        def _(s):
            parts = [landed[c, j, s] for j in range(chans)]
            qsend[c, s, 0] = (parts[0] + parts[1]) + (parts[2] + parts[3])
            scaled = [parts[j] * offs[j][0:1, :] for j in range(chans)]
            qsend[c, s, 1] = (scaled[0] + scaled[1]) + (scaled[2] + scaled[3])

        q_ref[c, slab] = qsend[c, slab]
        for d in range(1, slabs):
            q_copy(c, d, slab).start()

    def finish(c):
        for d in range(1, slabs):
            q_copy(c, d, slab_from(d)).wait_recv()
        at = pl.ds(pl.multiple_of(c * slabs * quarter, slabs * quarter), slabs * quarter)
        th, tl = xhigh_ref[at, :], xlow_ref[at, :]
        dot = functools.partial(jnp.dot, preferred_element_type=jnp.float32)
        for u0 in range(chans):
            held = jnp.concatenate(
                [
                    jnp.concatenate(
                        [
                            q_ref[c, s, t, pl.ds(u0, quarter, stride=chans), :]
                            for t in range(TERMS)
                        ],
                        axis=1,
                    )
                    for s in range(slabs)
                ],
                axis=0,
            )
            qh, ql = halves(held.T)
            acc[u0] += dot(qh, th) + (dot(ql, th) + dot(qh, tl))

    @pl.loop(0, CHUNKS + 4)
    def _(step):
        @pl.when(step < CHUNKS)
        def _():
            spread(step)

        @pl.when(jnp.logical_and(step >= 1, step < CHUNKS + 1))
        def _():
            weigh(step - 1)

        @pl.when(jnp.logical_and(step >= 3, step < CHUNKS + 3))
        def _():
            gather(step - 3)

        @pl.when(step >= 4)
        def _():
            finish(step - 4)

    for t in range(TERMS):
        @pl.loop(0, sub // GROUP)
        def _(i):
            rows = pl.ds(pl.multiple_of(i * GROUP, GROUP), GROUP)
            one = pl.ds(pl.multiple_of(t * lanes + i * GROUP, GROUP), GROUP)
            two = pl.ds(pl.multiple_of(t * lanes + half + i * GROUP, GROUP), GROUP)
            left, right = pl.ds(0, cols), pl.ds(cols, cols)
            real, imag = [], []
            for u0 in range(chans):
                cos, sin = turn_ref[2 * u0 : 2 * u0 + 1, :], turn_ref[2 * u0 + 1 : 2 * u0 + 2, :]
                yr = acc[u0, one, left] - acc[u0, two, right]
                yi = acc[u0, one, right] + acc[u0, two, left]
                real.append(yr * cos - yi * sin)
                imag.append(yr * sin + yi * cos)
            e0, e1 = real[0] + real[2], real[0] - real[2]
            o0, o1 = real[1] + real[3], imag[3] - imag[1]
            rsend[0, t, rows, :] = e0 + o0
            rsend[1, t, rows, :] = e1 + o1
            rsend[2, t, rows, :] = e0 - o0
            rsend[3, t, rows, :] = e1 - o1

    for d in range(1, chans):
        r_copy(d, chan).start()
    rrecv[chan] = rsend[chan]
    for d in range(1, chans):
        r_copy(d, chan_from(d)).wait_recv()
    for t in range(TERMS):
        for q in range(cols // lanes):
            at = pl.ds(q * lanes, lanes)
            for j in range(chans):
                stage[q, t, pl.ds(j, sub, stride=chans), :] = rrecv[j, t, :, at]
            out_ref[t, :, at] = stage[q, t]

    @pl.loop(0, CHUNKS)
    def _(c):
        for d in range(1, slabs):
            q_copy(c, d, slab).wait_send()
            z_copy(c, d, slab).wait_send()
        for d in range(1, chans):
            c_copy(c, d, chan).wait_send()
            b_copy(c, d, chan).wait_send()

    for d in range(1, chans):
        o_copy(d, chan).wait_send()
        x_copy(d, chan).wait_send()
        r_copy(d, chan).wait_send()


def local(taylor_models, gridded_vis, uv_weight, freq_ratio, robust_scale):
    chans = lax.axis_size("chan")
    slabs = lax.axis_size("slab")
    rows = taylor_models.shape[1]
    cols = taylor_models.shape[2]
    sub = rows // chans
    if slabs != 8 or chans != 4 or 2 * sub != 128:
        return local_general(taylor_models, gridded_vis, uv_weight, freq_ratio, robust_scale)
    unit = PIX // slabs // CHUNKS
    lanes = 2 * sub
    high, low = lane_tables(slabs, chans, sub)
    xhigh, xlow, turn = column_tables(slabs, chans, cols)
    vmem = pl.BlockSpec(memory_space=pltpu.VMEM)
    f32 = jnp.float32
    tile = (unit, lanes)
    piece = pltpu.VMEM((chans, TERMS, sub, cols), f32)
    operand = pltpu.VMEM((chans, TERMS * lanes, 2 * cols), jnp.bfloat16)
    columns = pltpu.VMEM((CHUNKS, slabs, TERMS) + tile, f32)
    wide = pltpu.VMEM((CHUNKS, chans, slabs) + tile, f32)
    others = pltpu.VMEM((CHUNKS, chans - 1, slabs) + tile, f32)
    sorted_tiles = pltpu.VMEM((CHUNKS, chans, unit, slabs * lanes), f32)
    return pl.pallas_call(
        functools.partial(middle_kernel, slabs, chans),
        out_shape=jax.ShapeDtypeStruct((TERMS, rows, cols), f32),
        in_specs=[vmem] * 11,
        out_specs=vmem,
        scratch_shapes=[
            pltpu.VMEM((cols // lanes, TERMS, rows, lanes), f32),
            piece, piece, operand, operand,
            pltpu.VMEM((chans, TERMS * lanes, 2 * cols), f32),
            piece, piece, columns, columns,
            columns, others, wide, others, wide, columns,
            pltpu.VMEM((chans, 8, lanes), f32),
            pltpu.VMEM((chans * slabs,) + tile, f32),
            sorted_tiles, sorted_tiles,
        ]
        + [pltpu.SemaphoreType.DMA((CHUNKS, slabs))] * 2
        + [pltpu.SemaphoreType.DMA((CHUNKS, chans))] * 4
        + [pltpu.SemaphoreType.DMA((CHUNKS, slabs))] * 2
        + [pltpu.SemaphoreType.DMA((chans,))] * 6,
        compiler_params=pltpu.CompilerParams(
            collective_id=0, has_side_effects=True, vmem_limit_bytes=63 * 1024 * 1024
        ),
    )(
        taylor_models, gridded_vis[0], uv_weight[0],
        jnp.broadcast_to(freq_ratio[0] - 1.0, (8, lanes)),
        jnp.broadcast_to(robust_scale[0], (8, lanes)),
        jnp.asarray(high), jnp.asarray(low), sort_table(slabs, sub),
        jnp.asarray(xhigh), jnp.asarray(xlow), jnp.asarray(turn),
    )


def solution(mesh):
    placed = (
        P(None, "slab", "chan"),
        P("chan", None, "slab", None),
        P("chan", "slab", None),
        P("chan"),
        P("chan"),
    )
    return jax.shard_map(
        local, mesh=mesh, in_specs=placed, out_specs=P(None, "slab", "chan"), check_vma=False
    )
```

profile of v0, /device:TPU:0, one launch (start us, length us, event | category | flops | bytes accessed | tf_op | source)
XLA Modules:
  0.0 192.1 jit_solution(7295262683799781376)
XLA Ops:
  1.3 0.6 broadcast_in_dim.8.off_ref
  1.9 0.6 broadcast_in_dim.9.rs_ref
  2.5 1.8 fusion.sort_ref
  4.3 185.6 %shard_map.100 = f32[2,256,512]{2,1,0:T(8,128)} custom-call(f32[2,256,512]{2,1,0:T(8,128)} %m_ref.1, bf16[2,256,2048]{2,1,0:T(8,128)(2,1)} %bitcast.5, bf16[256,2048]{1,0:T(8,128)(2,1)} %bitcast.6, f32[8,128]{1,0:T(8,128)} %broadcast_in_dim.8.off_ref, f32[8,128]{1,0:T(8,128)} %broadcast_in_dim.9.rs_ref, bf16[32,128,128]{2,1,0:T(8,128)(2,1)} %constant.69.clone.high_ref, ...), custom_call_target="tpu_custom_call" | custom-call | tf_op jit(solution)/shard_map/pallas_call | solution.py:569
  189.9 2.3 %copy.14 = f32[2,256,512]{2,1,0:T(8,128)} copy(f32[2,256,512]{2,1,0:T(8,128)} %shard_map.100) | data formatting | bytes 2097152
  (1 shorter events, 0.0 us)
where the time goes:
time: 195 us; the launch traced here: 192 us
  Pallas kernels  186 us (95%)
  local copies, waits for them, and re-layouts  3.45 us (2%)
    pallas_call x1, Pallas kernels, local(): pl.pallas_call(functools.partial(middle_kernel, slabs, chans), out_shape=...  186 us

commit v1 on v0

--- a/solution.py
+++ b/solution.py
@@ -173,20 +173,19 @@
     low = (table - high.astype(np.float32)).astype(jnp.bfloat16)
     turn = 2.0 * np.pi * np.arange(chans)[:, None] * np.arange(span)[None, :] / PIX
     turn = np.stack([np.cos(turn), np.sin(turn)], axis=1).reshape(2 * chans, span)
-    return high, low, turn.astype(np.float32)
+    parts = [x.reshape(CHUNKS, span // CHUNKS, 2 * span) for x in (high, low)]
+    return np.stack(parts, axis=1).reshape(2 * span, 2 * span), turn.astype(np.float32)
 
 
 def sort_table(slabs, sub):
-    span = slabs * sub
-    source = jnp.arange(2 * span, dtype=jnp.int32)
-    part, v = source // span, source % span
-    target = (v % slabs) * (2 * sub) + part * sub + v // slabs
-    return (target[:, None] == jnp.arange(2 * span, dtype=jnp.int32)[None, :]).astype(jnp.bfloat16)
+    source = jnp.arange(slabs * sub, dtype=jnp.int32)
+    target = (source % slabs) * sub + source // slabs
+    return (target[:, None] == source[None, :]).astype(jnp.bfloat16)
 
 
 def middle_kernel(
     slabs, chans, m_ref, vis_ref, wt_ref, off_ref, rs_ref, high_ref, low_ref, sort_ref,
-    xhigh_ref, xlow_ref, turn_ref, out_ref,
+    xtab_ref, turn_ref, out_ref,
     stage, xsend, xrecv, ohigh, olow, acc, rsend, rrecv, g_ref, q_ref, zin, mix, spec, back, landed, qsend, offs, work, vsort, wsort,
     z_send, z_recv, c_send, c_recv, b_send, b_recv, q_send, q_recv, o_send, o_recv,
     x_send, x_recv, r_send, r_recv,
@@ -278,15 +277,25 @@
     xrecv[chan] = xsend[chan]
     acc[...] = jnp.zeros_like(acc)
 
-    @pl.loop(0, CHUNKS)
-    def _(c):
-        rows = pl.ds(pl.multiple_of(c * unit, unit), unit)
-        for jj in range(chans):
-            at = pl.ds(jj * span, span)
-            pair = jnp.concatenate([vis_ref[0, rows, at], vis_ref[1, rows, at]], axis=1)
-            vsort[c, jj] = jnp.dot(pair, sort_ref[...], preferred_element_type=jnp.float32)
-            pair = jnp.concatenate([wt_ref[rows, at], wt_ref[rows, at]], axis=1)
-            wsort[c, jj] = jnp.dot(pair, sort_ref[...], preferred_element_type=jnp.float32)
+    @pl.loop(0, chans)
+    def _(jj):
+        at = pl.ds(pl.multiple_of(jj * span, span), span)
+        dot = functools.partial(jnp.dot, preferred_element_type=jnp.float32)
+        real, imag = dot(vis_ref[0, :, at], sort_ref[...]), dot(vis_ref[1, :, at], sort_ref[...])
+        scale = dot(wt_ref[:, at], sort_ref[...])
+        lower = lax.broadcasted_iota(jnp.int32, (unit, lanes), 1) < half
+        for c in range(CHUNKS):
+            for p in range(slabs // 2):
+                re, im, wt = [
+                    x[c * unit : (c + 1) * unit, p * lanes : (p + 1) * lanes]
+                    for x in (real, imag, scale)
+                ]
+                even, odd = pl.ds(2 * p * lanes, lanes), pl.ds((2 * p + 1) * lanes, lanes)
+                turned = pltpu.roll(wt, half, 1)
+                vsort[c, jj, :, even] = jnp.where(lower, re, pltpu.roll(im, half, 1))
+                vsort[c, jj, :, odd] = jnp.where(lower, pltpu.roll(re, half, 1), im)
+                wsort[c, jj, :, even] = jnp.where(lower, wt, turned)
+                wsort[c, jj, :, odd] = jnp.where(lower, turned, wt)
 
     for d in range(1, chans):
         o_copy(d, chan_from(d)).wait_recv()
@@ -325,13 +334,15 @@
 
     @pl.loop(0, CHUNKS)
     def _(c):
-        at = pl.ds(pl.multiple_of(c * slabs * quarter, slabs * quarter), slabs * quarter)
-        th, tl = xhigh_ref[at, :], xlow_ref[at, :]
+        count = slabs * quarter
+        at = pl.multiple_of(c * 2 * count, 2 * count)
+        both, wide = xtab_ref[pl.ds(at, 2 * count), :], xtab_ref[pl.ds(at, count), :]
         dot = functools.partial(
             lax.dot_general, dimension_numbers=(((1,), (1,)), ((), ())),
             preferred_element_type=jnp.float32)
         for u0 in range(chans):
-            found = dot(th, ohigh[u0]) + (dot(tl, ohigh[u0]) + dot(th, olow[u0]))
+            found = dot(both, ohigh[u0])
+            found = found[:count] + (found[count:] + dot(wide, olow[u0]))
             for s in range(slabs):
                 for m in range(TERMS):
                     g_ref[c, s, m, pl.ds(u0, quarter, stride=chans), :] = found[
@@ -372,8 +383,8 @@
         dot = functools.partial(
             lax.dot_general, dimension_numbers=(dims, ((), ())),
             preferred_element_type=jnp.float32)
-        wide = dot(high, high_ref[t])
-        return wide + (dot(low, high_ref[t]) + dot(high, low_ref[t]))
+        both = dot(jnp.concatenate([high, low], axis=0), high_ref[t])
+        return both[:unit] + (both[unit:] + dot(high, low_ref[t]))
 
     def spread(c):
         for d in range(1, slabs):
@@ -402,9 +413,12 @@
                 for v0 in range(slabs):
                     work[j * slabs + v0, rows, :] = out[v0]
 
-        @pl.loop(0, chans * slabs)
-        def _(t):
-            work[t] = product(work[t], t, ((1,), (0,)))
+        @pl.loop(0, chans)
+        def _(j):
+            tiles = [j * slabs + v0 for v0 in range(slabs)]
+            done = [product(work[t], t, ((1,), (0,))) for t in tiles]
+            for t, x in zip(tiles, done):
+                work[t] = x
 
         @pl.loop(0, unit // GROUP)
         def _(i):
@@ -422,9 +436,12 @@
                 for j in range(chans):
                     work[j * slabs + v0, rows, :] = out[j]
 
-        @pl.loop(0, chans * slabs)
-        def _(t):
-            work[t] = product(work[t], t, ((1,), (1,)))
+        @pl.loop(0, chans)
+        def _(j):
+            tiles = [j * slabs + v0 for v0 in range(slabs)]
+            done = [product(work[t], t, ((1,), (1,))) for t in tiles]
+            for t, x in zip(tiles, done):
+                work[t] = x
 
         @pl.loop(0, unit // GROUP)
         def _(i):
@@ -459,8 +476,9 @@
     def finish(c):
         for d in range(1, slabs):
             q_copy(c, d, slab_from(d)).wait_recv()
-        at = pl.ds(pl.multiple_of(c * slabs * quarter, slabs * quarter), slabs * quarter)
-        th, tl = xhigh_ref[at, :], xlow_ref[at, :]
+        count = slabs * quarter
+        at = pl.multiple_of(c * 2 * count, 2 * count)
+        th, tl = xtab_ref[pl.ds(at, count), :], xtab_ref[pl.ds(at + count, count), :]
         dot = functools.partial(jnp.dot, preferred_element_type=jnp.float32)
         for u0 in range(chans):
             held = jnp.concatenate(
@@ -477,7 +495,8 @@
                 axis=0,
             )
             qh, ql = halves(held.T)
-            acc[u0] += dot(qh, th) + (dot(ql, th) + dot(qh, tl))
+            found = dot(jnp.concatenate([qh, ql], axis=0), th)
+            acc[u0] += found[: TERMS * lanes] + (found[TERMS * lanes :] + dot(qh, tl))
 
     @pl.loop(0, CHUNKS + 4)
     def _(step):
@@ -556,7 +575,7 @@
     unit = PIX // slabs // CHUNKS
     lanes = 2 * sub
     high, low = lane_tables(slabs, chans, sub)
-    xhigh, xlow, turn = column_tables(slabs, chans, cols)
+    xtab, turn = column_tables(slabs, chans, cols)
     vmem = pl.BlockSpec(memory_space=pltpu.VMEM)
     f32 = jnp.float32
     tile = (unit, lanes)
@@ -569,7 +588,7 @@
     return pl.pallas_call(
         functools.partial(middle_kernel, slabs, chans),
         out_shape=jax.ShapeDtypeStruct((TERMS, rows, cols), f32),
-        in_specs=[vmem] * 11,
+        in_specs=[vmem] * 10,
         out_specs=vmem,
         scratch_shapes=[
             pltpu.VMEM((cols // lanes, TERMS, rows, lanes), f32),
@@ -593,7 +612,7 @@
         jnp.broadcast_to(freq_ratio[0] - 1.0, (8, lanes)),
         jnp.broadcast_to(robust_scale[0], (8, lanes)),
         jnp.asarray(high), jnp.asarray(low), sort_table(slabs, sub),
-        jnp.asarray(xhigh), jnp.asarray(xlow), jnp.asarray(turn),
+        jnp.asarray(xtab), jnp.asarray(turn),
     )
 
 

time: 195 us -> 180 us (0.923)
  Pallas kernels: 186 us -> 171 us
    pallas_call x1, Pallas kernels: 186 us -> 171 us  [local(): pl.pallas_call(functools.partial(middle_kernel, slabs, chans), out_shape=...]
where the time goes in v1:
time: 180 us; the launch traced here: 177 us
  Pallas kernels  171 us (95%)
  local copies, waits for them, and re-layouts  3.45 us (2%)
    pallas_call x1, Pallas kernels, local(): pl.pallas_call(functools.partial(middle_kernel, slabs, chans), out_shape=...  171 us

profile of v1, /device:TPU:0, one launch (start us, length us, event | category | flops | bytes accessed | tf_op | source)
XLA Modules:
  0.0 177.1 jit_solution(8022533803766168145)
XLA Ops:
  1.3 0.6 broadcast_in_dim.8.off_ref
  1.9 0.6 broadcast_in_dim.9.rs_ref
  2.5 0.9 fusion.sort_ref
  3.4 171.4 %shard_map.91 = f32[2,256,512]{2,1,0:T(8,128)} custom-call(f32[2,256,512]{2,1,0:T(8,128)} %m_ref.1, bf16[2,256,2048]{2,1,0:T(8,128)(2,1)} %bitcast.5, bf16[256,2048]{1,0:T(8,128)(2,1)} %bitcast.6, f32[8,128]{1,0:T(8,128)} %broadcast_in_dim.8.off_ref, f32[8,128]{1,0:T(8,128)} %broadcast_in_dim.9.rs_ref, bf16[32,128,128]{2,1,0:T(8,128)(2,1)} %constant.45.clone.high_ref, ...), custom_call_target="tpu_custom_call" | custom-call | tf_op jit(solution)/shard_map/pallas_call | solution.py:588
  174.9 2.3 %copy.13 = f32[2,256,512]{2,1,0:T(8,128)} copy(f32[2,256,512]{2,1,0:T(8,128)} %shard_map.91) | data formatting | bytes 2097152
  (1 shorter events, 0.0 us)

commit v2 on v1

--- a/solution.py
+++ b/solution.py
@@ -143,7 +143,7 @@
     return tiles.transpose(1, 0, 2, 3).reshape(TERMS, rows, cols)
 
 
-CHUNKS = 4
+CHUNKS = 8
 GROUP = 8
 MESH = pl.DeviceIdType.MESH
 

time: 180 us -> 167 us (0.928); the launches traced: 177 us -> 166 us
  Pallas kernels: 171 us -> 161 us
    pallas_call x1, Pallas kernels: 171 us -> 161 us  [local(): pl.pallas_call(functools.partial(middle_kernel, slabs, chans), out_shape=...]
where the time goes in v2:
time: 167 us; the launch traced here: 166 us
  Pallas kernels  161 us (96%)
  local copies, waits for them, and re-layouts  3.45 us (2%)
    pallas_call x1, Pallas kernels, local(): pl.pallas_call(functools.partial(middle_kernel, slabs, chans), out_shape=...  161 us

profile of v2, /device:TPU:0, one launch (start us, length us, event | category | flops | bytes accessed | tf_op | source)
XLA Modules:
  0.0 166.4 jit_solution(17492853044359547002)
XLA Ops:
  1.3 0.6 broadcast_in_dim.8.off_ref
  1.9 0.6 broadcast_in_dim.9.rs_ref
  2.5 0.9 fusion.sort_ref
  3.4 160.7 %shard_map.91 = f32[2,256,512]{2,1,0:T(8,128)} custom-call(f32[2,256,512]{2,1,0:T(8,128)} %m_ref.1, bf16[2,256,2048]{2,1,0:T(8,128)(2,1)} %bitcast.5, bf16[256,2048]{1,0:T(8,128)(2,1)} %bitcast.6, f32[8,128]{1,0:T(8,128)} %broadcast_in_dim.8.off_ref, f32[8,128]{1,0:T(8,128)} %broadcast_in_dim.9.rs_ref, bf16[32,128,128]{2,1,0:T(8,128)(2,1)} %constant.45.clone.high_ref, ...), custom_call_target="tpu_custom_call" | custom-call | tf_op jit(solution)/shard_map/pallas_call | solution.py:588
  164.1 2.3 %copy.13 = f32[2,256,512]{2,1,0:T(8,128)} copy(f32[2,256,512]{2,1,0:T(8,128)} %shard_map.91) | data formatting | bytes 2097152
  (1 shorter events, 0.0 us)
